TPU v7x, 32 devices: a whole 2x2x4 slice. The times are simulated.
32 devices in a mesh: gx: 4 (over z), gy: 8 (over y, x, core).
Axes of the slice: x: 2, y: 2, z: 4, core: 2. Of those that a mesh axis runs over, the one named last changes fastest.
Arguments:
- substrates: float32 [8, 256, 128, 128], P(None, 'gx', 'gy'), may hold values from 0 to 2
- uptake: float32 [256, 128, 128], P('gx', 'gy'), may hold values from 0.5 to 2
- diffusion: float32 [8], replicated, may hold values from 0.1 to 0.15
- decay_rate: float32 [8], replicated, may hold values from 0.01 to 0.1
Outputs:
- advanced: float32 [8, 256, 128, 128], P(None, 'gx', 'gy')
All inputs are finite; a program needn't handle non-finite values.
Results may differ from a plain program's by a relative error of at most 0.00002.
Values sent between devices are 32-bit elements; how exact they have to be, the bound alone decides.
A program may use at most 128 MiB of HBM per device.

v0:
```python
import functools

import jax
import jax.numpy as jnp
from jax import lax
from jax.experimental import pallas as pl
from jax.experimental.pallas import tpu as pltpu
from jax.sharding import PartitionSpec as P

SUBSTEPS = 4
PITCH_PAD = 16
Y0 = 8
MESH = pl.DeviceIdType.MESH


def kernel(
    n_x, n_y, sub_ref, up_ref, dif_hbm, dec_hbm, out_ref,
    field, uptake, result, faces, halos, load_sem, up_sem, store_sem, send_sem, recv_sem,
    dif_ref, dec_ref, scalar_sem,
):
    count, cx, cy, cz = sub_ref.shape
    pitch = cy + PITCH_PAD
    rows = field.reshape(SUBSTEPS, count, (cx + 2) * pitch, cz)
    gx, gy = lax.axis_index("gx"), lax.axis_index("gy")
    low_x, high_x = lax.rem(gx + n_x - 1, n_x), lax.rem(gx + 1, n_x)
    low_y, high_y = lax.rem(gy + n_y - 1, n_y), lax.rem(gy + 1, n_y)
    inner = pl.ds(Y0, cy)

    def load(s):
        return pltpu.make_async_copy(
            sub_ref.at[s], field.at[0, s, pl.ds(1, cx), inner, :], load_sem.at[s]
        )

    def store(s):
        return pltpu.make_async_copy(result.at[s], out_ref.at[s], store_sem.at[s])

    def sends(t, s):
        here = field.at[t, s]
        pairs = (
            (faces.at[t, s, 0], halos.at[t, s, 0], (gx, low_y)),
            (faces.at[t, s, 1], halos.at[t, s, 1], (gx, high_y)),
            (here.at[1, inner, :], here.at[cx + 1, inner, :], (low_x, gy)),
            (here.at[cx, inner, :], here.at[0, inner, :], (high_x, gy)),
        )
        return [
            pltpu.make_async_remote_copy(
                src_ref=src, dst_ref=dst, send_sem=send_sem.at[t, s, k],
                recv_sem=recv_sem.at[t, s, k], device_id=target, device_id_type=MESH,
            )
            for k, (src, dst, target) in enumerate(pairs)
        ]

    def emit(t, s):
        for i in range(cx // 8):
            top = (1 + 8 * i) * pitch + Y0
            faces[t, s, 0, pl.ds(8 * i, 8), :] = rows[t, s, pl.ds(top, 8, stride=pitch), :]
            faces[t, s, 1, pl.ds(8 * i, 8), :] = rows[
                t, s, pl.ds(top + cy - 1, 8, stride=pitch), :
            ]
        for copy in sends(t, s):
            copy.start()

    def unit(t, s):
        for copy in sends(t, s):
            copy.wait_recv()
        for i in range(cx // 8):
            top = (1 + 8 * i) * pitch + Y0
            rows[t, s, pl.ds(top + cy, 8, stride=pitch), :] = halos[t, s, 0, pl.ds(8 * i, 8), :]
            rows[t, s, pl.ds(top - 1, 8, stride=pitch), :] = halos[t, s, 1, pl.ds(8 * i, 8), :]
        diffuse = dif_ref[s]
        keep = 1.0 - 6.0 * diffuse
        decay = dec_ref[s]
        block = cx

        def strip(b, carry):
            x0 = b * block
            for y in range(0, cy, 8):
                below = field[t, s, x0, pl.ds(Y0 + y, 8), :]
                center = field[t, s, x0 + 1, pl.ds(Y0 + y, 8), :]
                for i in range(block):
                    x = x0 + i
                    above = field[t, s, x + 2, pl.ds(Y0 + y, 8), :]
                    total = below + above
                    total = total + (
                        field[t, s, x + 1, pl.ds(Y0 + y - 1, 8), :]
                        + field[t, s, x + 1, pl.ds(Y0 + y + 1, 8), :]
                    )
                    total = total + (pltpu.roll(center, 1, 1) + pltpu.roll(center, cz - 1, 1))
                    factor = keep - decay * uptake[x, pl.ds(y, 8), :]
                    value = diffuse * total + factor * center
                    if t + 1 < SUBSTEPS:
                        field[t + 1, s, x + 1, pl.ds(Y0 + y, 8), :] = value
                    else:
                        result[s, x, pl.ds(y, 8), :] = value
                    below, center = center, above
            return carry

        lax.fori_loop(0, cx // block, strip, 0)

    each = functools.partial(lax.fori_loop, 0, count, init_val=0)

    def run(body):
        def wrapped(s, carry):
            body(s)
            return carry

        each(body_fun=wrapped)

    run(lambda s: load(s).start())
    up_copy = pltpu.make_async_copy(up_ref, uptake, up_sem)
    up_copy.start()
    scalar_copies = [
        pltpu.make_async_copy(dif_hbm, dif_ref, scalar_sem.at[0]),
        pltpu.make_async_copy(dec_hbm, dec_ref, scalar_sem.at[1]),
    ]
    for copy in scalar_copies:
        copy.start()
    barrier = pltpu.get_barrier_semaphore()
    for target in ((gx, low_y), (gx, high_y), (low_x, gy), (high_x, gy)):
        pl.semaphore_signal(barrier, inc=1, device_id=target, device_id_type=MESH)
    pl.semaphore_wait(barrier, 4)

    def first(s):
        load(s).wait()
        emit(0, s)

    run(first)
    up_copy.wait()
    for copy in scalar_copies:
        copy.wait()
    for t in range(SUBSTEPS):

        def advance(s):
            unit(t, s)
            if t + 1 < SUBSTEPS:
                emit(t + 1, s)
            else:
                store(s).start()

        run(advance)

    def finish(s):
        for t in range(SUBSTEPS):
            for copy in sends(t, s):
                copy.wait_send()
        store(s).wait()

    run(finish)


def solution(mesh):
    n_x, n_y = mesh.shape["gx"], mesh.shape["gy"]

    def local(substrates, uptake, diffusion, decay_rate):
        count, cx, cy, cz = substrates.shape
        any_spec = pl.BlockSpec(memory_space=pl.ANY)
        hbm_spec = pl.BlockSpec(memory_space=pltpu.HBM)
        return pl.pallas_call(
            functools.partial(kernel, n_x, n_y),
            out_shape=jax.ShapeDtypeStruct(substrates.shape, substrates.dtype),
            in_specs=[hbm_spec] * 4,
            out_specs=any_spec,
            scratch_shapes=[
                pltpu.VMEM((SUBSTEPS, count, cx + 2, cy + PITCH_PAD, cz), jnp.float32),
                pltpu.VMEM((cx, cy, cz), jnp.float32),
                pltpu.VMEM((count, cx, cy, cz), jnp.float32),
                pltpu.VMEM((SUBSTEPS, count, 2, cx, cz), jnp.float32),
                pltpu.VMEM((SUBSTEPS, count, 2, cx, cz), jnp.float32),
                pltpu.SemaphoreType.DMA((count,)),
                pltpu.SemaphoreType.DMA,
                pltpu.SemaphoreType.DMA((count,)),
                pltpu.SemaphoreType.DMA((SUBSTEPS, count, 4)),
                pltpu.SemaphoreType.DMA((SUBSTEPS, count, 4)),
                pltpu.SMEM((count,), jnp.float32),
                pltpu.SMEM((count,), jnp.float32),
                pltpu.SemaphoreType.DMA((2,)),
            ],
            compiler_params=pltpu.CompilerParams(
                collective_id=0, has_side_effects=True, vmem_limit_bytes=47 * 1024 * 1024
            ),
        )(*[pltpu.with_memory_space_constraint(v, pltpu.HBM) for v in (substrates, uptake, diffusion, decay_rate)])

    placed = (P(None, "gx", "gy", None), P("gx", "gy", None), P(), P())
    return jax.shard_map(
        local, mesh=mesh, in_specs=placed, out_specs=P(None, "gx", "gy", None), check_vma=False
    )
```

profile of v0, /device:TPU:0, one launch (start us, length us, event | category | flops | bytes accessed | tf_op | source)
XLA Modules:
  0.0 34.4 jit_solution(11738133498252034431)
XLA Ops:
  0.0 32.4 %shard_map.46 = f32[8,64,16,128]{3,2,1,0:T(8,128)S(1)} custom-call(f32[8,64,16,128]{3,2,1,0:T(8,128)} %sub_ref.1, f32[64,16,128]{2,1,0:T(8,128)} %up_ref.1, f32[8]{0:T(128)} %dif_hbm.1, f32[8]{0:T(128)} %dec_hbm.1), custom_call_target="tpu_custom_call" | custom-call | tf_op jit(solution)/shard_map/pallas_call | solution.py:158
  32.4 2.0 %copy.6 = f32[8,64,16,128]{3,2,1,0:T(8,128)} copy(f32[8,64,16,128]{3,2,1,0:T(8,128)S(1)} %shard_map.46) | data formatting | bytes 8388608
where the time goes:
time: 34.6 us; the launch traced here: 34.4 us
  Pallas kernels  32.4 us (94%)
  local copies, waits for them, and re-layouts  2.02 us (6%)
    pallas_call x1, Pallas kernels, local(): pl.pallas_call(functools.partial(kernel, n_x, n_y), out_shape=jax.ShapeDt...  32.4 us
    unnamed x1, local copies, waits for them, and re-layouts  2.02 us

commit v1 on v0

v1 whole, which is shorter than its diff:
```python
import functools

import jax
import jax.numpy as jnp
from jax import lax
from jax.experimental import pallas as pl
from jax.experimental.pallas import tpu as pltpu
from jax.sharding import PartitionSpec as P

SUBSTEPS = 4
PITCH_PAD = 16
Y0 = 8
EARLY = 2
MESH = pl.DeviceIdType.MESH


def kernel(
    n_x, n_y, sub_ref, up_ref, dif_hbm, dec_hbm, out_ref,
    field, uptake, faces, halos, load_sem, up_sem, send_sem, recv_sem,
    dif_ref, dec_ref, scalar_sem, ready,
):
    count, cx, cy, cz = sub_ref.shape
    pitch = cy + PITCH_PAD
    rows = field.reshape(SUBSTEPS, count, (cx + 2) * pitch, cz)
    gx, gy = lax.axis_index("gx"), lax.axis_index("gy")
    low_x, high_x = lax.rem(gx + n_x - 1, n_x), lax.rem(gx + 1, n_x)
    low_y, high_y = lax.rem(gy + n_y - 1, n_y), lax.rem(gy + 1, n_y)
    inner = pl.ds(Y0, cy)
    along_x = (low_x, high_x)

    def load(s):
        return pltpu.make_async_copy(
            sub_ref.at[s], field.at[0, s, pl.ds(1, cx), inner, :], load_sem.at[s]
        )

    def remote(t, s, k, src, dst, target):
        return pltpu.make_async_remote_copy(
            src_ref=src, dst_ref=dst, send_sem=send_sem.at[t, s, k],
            recv_sem=recv_sem.at[t, s, k], device_id=target, device_id_type=MESH,
        )

    def y_sends(t, s):
        return [
            remote(t, s, 0, faces.at[t, s, 0], halos.at[t, s, 0], (gx, low_y)),
            remote(t, s, 1, faces.at[t, s, 1], halos.at[t, s, 1], (gx, high_y)),
        ]

    def x_sends(t, s):
        here = field.at[t, s]
        return [
            remote(t, s, 2, here.at[1, inner, :], here.at[cx + 1, inner, :], (low_x, gy)),
            remote(t, s, 3, here.at[cx, inner, :], here.at[0, inner, :], (high_x, gy)),
        ]

    def sends(t, s):
        return y_sends(t, s) + x_sends(t, s)

    def make_faces(t, s):
        for i in range(cx // 8):
            top = (1 + 8 * i) * pitch + Y0
            faces[t, s, 0, pl.ds(8 * i, 8), :] = rows[t, s, pl.ds(top, 8, stride=pitch), :]
            faces[t, s, 1, pl.ds(8 * i, 8), :] = rows[
                t, s, pl.ds(top + cy - 1, 8, stride=pitch), :
            ]

    def unit(t, s):
        for copy in sends(t, s):
            copy.wait_recv()
        for i in range(cx // 8):
            top = (1 + 8 * i) * pitch + Y0
            rows[t, s, pl.ds(top + cy, 8, stride=pitch), :] = halos[t, s, 0, pl.ds(8 * i, 8), :]
            rows[t, s, pl.ds(top - 1, 8, stride=pitch), :] = halos[t, s, 1, pl.ds(8 * i, 8), :]
        diffuse = dif_ref[s]
        keep = 1.0 - 6.0 * diffuse
        decay = dec_ref[s]
        for y in range(0, cy, 8):
            below = field[t, s, 0, pl.ds(Y0 + y, 8), :]
            center = field[t, s, 1, pl.ds(Y0 + y, 8), :]
            for x in range(cx):
                above = field[t, s, x + 2, pl.ds(Y0 + y, 8), :]
                total = below + above
                total = total + (
                    field[t, s, x + 1, pl.ds(Y0 + y - 1, 8), :]
                    + field[t, s, x + 1, pl.ds(Y0 + y + 1, 8), :]
                )
                total = total + (pltpu.roll(center, 1, 1) + pltpu.roll(center, cz - 1, 1))
                factor = keep - decay * uptake[x, pl.ds(y, 8), :]
                value = diffuse * total + factor * center
                if t + 1 < SUBSTEPS:
                    field[t + 1, s, x + 1, pl.ds(Y0 + y, 8), :] = value
                else:
                    out_ref[s, x, pl.ds(y, 8), :] = value
                below, center = center, above

    def run(first, last, body):
        def wrapped(s, carry):
            body(s)
            return carry

        lax.fori_loop(first, last, wrapped, 0)

    barrier = pltpu.get_barrier_semaphore()
    for target in ((gx, low_y), (gx, high_y)):
        pl.semaphore_signal(barrier, inc=1, device_id=target, device_id_type=MESH)
    for other in along_x:

        @pl.when(other > gx)
        def _():
            pl.semaphore_signal(barrier, inc=1, device_id=(other, gy), device_id_type=MESH)

    run(0, count, lambda s: load(s).start())
    up_copy = pltpu.make_async_copy(up_ref, uptake, up_sem)
    up_copy.start()
    scalar_copies = [
        pltpu.make_async_copy(dif_hbm, dif_ref, scalar_sem.at[0]),
        pltpu.make_async_copy(dec_hbm, dec_ref, scalar_sem.at[1]),
    ]
    for copy in scalar_copies:
        copy.start()

    def fetch(s):
        load(s).wait()
        make_faces(0, s)

    def launch(s):
        for copy in y_sends(0, s):
            copy.start()
        for other, copy in zip(along_x, x_sends(0, s)):

            @pl.when(other < gx)
            def _():
                copy.start()

    run(0, EARLY, fetch)
    n_lower = sum((other < gx).astype(jnp.int32) for other in along_x)
    pl.semaphore_wait(barrier, 2 + n_lower)
    for k, other in enumerate(along_x):

        @pl.when(other < gx)
        def _():
            pl.semaphore_signal(
                ready.at[1 - k], inc=1, device_id=(other, gy), device_id_type=MESH
            )

    run(0, EARLY, launch)

    def fetch_and_launch(s):
        fetch(s)
        launch(s)

    run(EARLY, count, fetch_and_launch)
    for k, other in enumerate(along_x):

        @pl.when(other > gx)
        def _():
            pl.semaphore_wait(ready.at[k], 1)
            run(0, count, lambda s: x_sends(0, s)[k].start())

    up_copy.wait()
    for copy in scalar_copies:
        copy.wait()
    for t in range(SUBSTEPS):

        def advance(s):
            unit(t, s)
            if t + 1 < SUBSTEPS:
                make_faces(t + 1, s)
                for copy in sends(t + 1, s):
                    copy.start()
            if t > 0:
                for copy in sends(t - 1, s):
                    copy.wait_send()

        run(0, count, advance)

    def finish(s):
        for copy in sends(SUBSTEPS - 1, s):
            copy.wait_send()

    run(0, count, finish)


def solution(mesh):
    n_x, n_y = mesh.shape["gx"], mesh.shape["gy"]

    def local(substrates, uptake, diffusion, decay_rate):
        count, cx, cy, cz = substrates.shape
        hbm_spec = pl.BlockSpec(memory_space=pltpu.HBM)
        return pl.pallas_call(
            functools.partial(kernel, n_x, n_y),
            out_shape=jax.ShapeDtypeStruct(substrates.shape, substrates.dtype),
            in_specs=[hbm_spec] * 4,
            out_specs=pl.BlockSpec(memory_space=pltpu.VMEM),
            scratch_shapes=[
                pltpu.VMEM((SUBSTEPS, count, cx + 2, cy + PITCH_PAD, cz), jnp.float32),
                pltpu.VMEM((cx, cy, cz), jnp.float32),
                pltpu.VMEM((SUBSTEPS, count, 2, cx, cz), jnp.float32),
                pltpu.VMEM((SUBSTEPS, count, 2, cx, cz), jnp.float32),
                pltpu.SemaphoreType.DMA((count,)),
                pltpu.SemaphoreType.DMA,
                pltpu.SemaphoreType.DMA((SUBSTEPS, count, 4)),
                pltpu.SemaphoreType.DMA((SUBSTEPS, count, 4)),
                pltpu.SMEM((count,), jnp.float32),
                pltpu.SMEM((count,), jnp.float32),
                pltpu.SemaphoreType.DMA((2,)),
                pltpu.SemaphoreType.REGULAR((2,)),
            ],
            compiler_params=pltpu.CompilerParams(
                collective_id=0, has_side_effects=True, vmem_limit_bytes=44 * 1024 * 1024
            ),
        )(*[pltpu.with_memory_space_constraint(v, pltpu.HBM) for v in (substrates, uptake, diffusion, decay_rate)])

    placed = (P(None, "gx", "gy", None), P("gx", "gy", None), P(), P())
    return jax.shard_map(
        local, mesh=mesh, in_specs=placed, out_specs=P(None, "gx", "gy", None), check_vma=False
    )
```

time: 34.6 us -> 32.5 us (0.939)
  Pallas kernels: 32.4 us -> 30.2 us
    pallas_call x1, Pallas kernels: 32.4 us -> 30.2 us  [local(): pl.pallas_call(functools.partial(kernel, n_x, n_y), out_shape=jax.ShapeDt...]
where the time goes in v1:
time: 32.5 us; the launch traced here: 32.2 us
  Pallas kernels  30.2 us (93%)
  local copies, waits for them, and re-layouts  2.02 us (6%)
    pallas_call x1, Pallas kernels, local(): pl.pallas_call(functools.partial(kernel, n_x, n_y), out_shape=jax.ShapeDt...  30.2 us
    unnamed x1, local copies, waits for them, and re-layouts  2.02 us

profile of v1, /device:TPU:0, one launch (start us, length us, event | category | flops | bytes accessed | tf_op | source)
XLA Modules:
  0.0 32.2 jit_solution(9881719368831321933)
XLA Ops:
  0.0 30.2 %shard_map.46 = f32[8,64,16,128]{3,2,1,0:T(8,128)S(1)} custom-call(f32[8,64,16,128]{3,2,1,0:T(8,128)} %sub_ref.1, f32[64,16,128]{2,1,0:T(8,128)} %up_ref.1, f32[8]{0:T(128)} %dif_hbm.1, f32[8]{0:T(128)} %dec_hbm.1), custom_call_target="tpu_custom_call" | custom-call | tf_op jit(solution)/shard_map/pallas_call | solution.py:189
  30.2 2.0 %copy.6 = f32[8,64,16,128]{3,2,1,0:T(8,128)} copy(f32[8,64,16,128]{3,2,1,0:T(8,128)S(1)} %shard_map.46) | data formatting | bytes 8388608

commit v2 on v1

--- a/solution.py
+++ b/solution.py
@@ -16,7 +16,7 @@
 
 def kernel(
     n_x, n_y, sub_ref, up_ref, dif_hbm, dec_hbm, out_ref,
-    field, uptake, faces, halos, load_sem, up_sem, send_sem, recv_sem,
+    field, uptake, faces, halos, front_sem, bulk_sem, up_sem, send_sem, recv_sem,
     dif_ref, dec_ref, scalar_sem, ready,
 ):
     count, cx, cy, cz = sub_ref.shape
@@ -28,32 +28,47 @@
     inner = pl.ds(Y0, cy)
     along_x = (low_x, high_x)
 
-    def load(s):
+    shell = 2 * (cx + cy)
+    flat = field.reshape(SUBSTEPS * count * (cx + 2) * pitch, cz)
+
+    def front(s, group):
+        pairs = (
+            (sub_ref.at[s, :, 0, :], faces.at[0, s, 0]),
+            (sub_ref.at[s, :, cy - 1, :], faces.at[0, s, 1]),
+            (sub_ref.at[s, 0], field.at[0, s, 1, inner, :]),
+            (sub_ref.at[s, cx - 1], field.at[0, s, cx, inner, :]),
+        )
+        return [pltpu.make_async_copy(src, dst, front_sem.at[group]) for src, dst in pairs]
+
+    def bulk(s):
         return pltpu.make_async_copy(
-            sub_ref.at[s], field.at[0, s, pl.ds(1, cx), inner, :], load_sem.at[s]
+            sub_ref.at[s, pl.ds(1, cx - 2)], field.at[0, s, pl.ds(2, cx - 2), inner, :], bulk_sem
         )
 
-    def remote(t, s, k, src, dst, target):
+    def await_rows(n, sem):
+        span = flat.at[pl.ds(0, n), :]
+        pltpu.make_async_copy(span, span, sem).wait()
+
+    def remote(t, s, src, dst, target):
         return pltpu.make_async_remote_copy(
-            src_ref=src, dst_ref=dst, send_sem=send_sem.at[t, s, k],
-            recv_sem=recv_sem.at[t, s, k], device_id=target, device_id_type=MESH,
+            src_ref=src, dst_ref=dst, send_sem=send_sem.at[t],
+            recv_sem=recv_sem.at[t % 2, s], device_id=target, device_id_type=MESH,
         )
 
     def y_sends(t, s):
         return [
-            remote(t, s, 0, faces.at[t, s, 0], halos.at[t, s, 0], (gx, low_y)),
-            remote(t, s, 1, faces.at[t, s, 1], halos.at[t, s, 1], (gx, high_y)),
+            remote(t, s, faces.at[t, s, 0], halos.at[t, s, 0], (gx, low_y)),
+            remote(t, s, faces.at[t, s, 1], halos.at[t, s, 1], (gx, high_y)),
         ]
 
-    def x_sends(t, s):
+    def x_send(t, s, k):
         here = field.at[t, s]
-        return [
-            remote(t, s, 2, here.at[1, inner, :], here.at[cx + 1, inner, :], (low_x, gy)),
-            remote(t, s, 3, here.at[cx, inner, :], here.at[0, inner, :], (high_x, gy)),
-        ]
+        if k == 0:
+            return remote(t, s, here.at[1, inner, :], here.at[cx + 1, inner, :], (low_x, gy))
+        return remote(t, s, here.at[cx, inner, :], here.at[0, inner, :], (high_x, gy))
 
     def sends(t, s):
-        return y_sends(t, s) + x_sends(t, s)
+        return y_sends(t, s) + [x_send(t, s, 0), x_send(t, s, 1)]
 
     def make_faces(t, s):
         for i in range(cx // 8):
@@ -64,8 +79,7 @@
             ]
 
     def unit(t, s):
-        for copy in sends(t, s):
-            copy.wait_recv()
+        await_rows(shell, recv_sem.at[t % 2, s])
         for i in range(cx // 8):
             top = (1 + 8 * i) * pitch + Y0
             rows[t, s, pl.ds(top + cy, 8, stride=pitch), :] = halos[t, s, 0, pl.ds(8 * i, 8), :]
@@ -108,30 +122,32 @@
         def _():
             pl.semaphore_signal(barrier, inc=1, device_id=(other, gy), device_id_type=MESH)
 
-    run(0, count, lambda s: load(s).start())
-    up_copy = pltpu.make_async_copy(up_ref, uptake, up_sem)
-    up_copy.start()
+    for first, last, group in ((0, EARLY, 0), (EARLY, count, 1)):
+
+        def begin(s):
+            for copy in front(s, group):
+                copy.start()
+
+        run(first, last, begin)
     scalar_copies = [
         pltpu.make_async_copy(dif_hbm, dif_ref, scalar_sem.at[0]),
         pltpu.make_async_copy(dec_hbm, dec_ref, scalar_sem.at[1]),
     ]
     for copy in scalar_copies:
         copy.start()
-
-    def fetch(s):
-        load(s).wait()
-        make_faces(0, s)
+    run(0, count, lambda s: bulk(s).start())
+    up_copy = pltpu.make_async_copy(up_ref, uptake, up_sem)
+    up_copy.start()
 
     def launch(s):
         for copy in y_sends(0, s):
             copy.start()
-        for other, copy in zip(along_x, x_sends(0, s)):
+        for k, other in enumerate(along_x):
 
             @pl.when(other < gx)
             def _():
-                copy.start()
-
-    run(0, EARLY, fetch)
+                x_send(0, s, k).start()
+
     n_lower = sum((other < gx).astype(jnp.int32) for other in along_x)
     pl.semaphore_wait(barrier, 2 + n_lower)
     for k, other in enumerate(along_x):
@@ -142,20 +158,17 @@
                 ready.at[1 - k], inc=1, device_id=(other, gy), device_id_type=MESH
             )
 
-    run(0, EARLY, launch)
-
-    def fetch_and_launch(s):
-        fetch(s)
-        launch(s)
-
-    run(EARLY, count, fetch_and_launch)
+    for first, last, group in ((0, EARLY, 0), (EARLY, count, 1)):
+        await_rows((last - first) * shell, front_sem.at[group])
+        run(first, last, launch)
     for k, other in enumerate(along_x):
 
         @pl.when(other > gx)
         def _():
             pl.semaphore_wait(ready.at[k], 1)
-            run(0, count, lambda s: x_sends(0, s)[k].start())
-
+            run(0, count, lambda s: x_send(0, s, k).start())
+
+    await_rows(count * (cx - 2) * cy, bulk_sem)
     up_copy.wait()
     for copy in scalar_copies:
         copy.wait()
@@ -167,17 +180,11 @@
                 make_faces(t + 1, s)
                 for copy in sends(t + 1, s):
                     copy.start()
-            if t > 0:
-                for copy in sends(t - 1, s):
-                    copy.wait_send()
 
         run(0, count, advance)
 
-    def finish(s):
-        for copy in sends(SUBSTEPS - 1, s):
-            copy.wait_send()
-
-    run(0, count, finish)
+    for t in range(SUBSTEPS):
+        await_rows(count * shell, send_sem.at[t])
 
 
 def solution(mesh):
@@ -196,10 +203,11 @@
                 pltpu.VMEM((cx, cy, cz), jnp.float32),
                 pltpu.VMEM((SUBSTEPS, count, 2, cx, cz), jnp.float32),
                 pltpu.VMEM((SUBSTEPS, count, 2, cx, cz), jnp.float32),
-                pltpu.SemaphoreType.DMA((count,)),
+                pltpu.SemaphoreType.DMA((2,)),
                 pltpu.SemaphoreType.DMA,
-                pltpu.SemaphoreType.DMA((SUBSTEPS, count, 4)),
-                pltpu.SemaphoreType.DMA((SUBSTEPS, count, 4)),
+                pltpu.SemaphoreType.DMA,
+                pltpu.SemaphoreType.DMA((SUBSTEPS,)),
+                pltpu.SemaphoreType.DMA((2, count)),
                 pltpu.SMEM((count,), jnp.float32),
                 pltpu.SMEM((count,), jnp.float32),
                 pltpu.SemaphoreType.DMA((2,)),

time: 32.5 us -> 30.3 us (0.932)
  Pallas kernels: 30.2 us -> 28 us
    pallas_call x1, Pallas kernels: 30.2 us -> 28 us  [local(): pl.pallas_call(functools.partial(kernel, n_x, n_y), out_shape=jax.ShapeDt...]
where the time goes in v2:
time: 30.3 us; the launch traced here: 30 us
  Pallas kernels  28 us (92%)
  local copies, waits for them, and re-layouts  2.02 us (7%)
    pallas_call x1, Pallas kernels, local(): pl.pallas_call(functools.partial(kernel, n_x, n_y), out_shape=jax.ShapeDt...  28 us
    unnamed x1, local copies, waits for them, and re-layouts  2.02 us

profile of v2, /device:TPU:0, one launch (start us, length us, event | category | flops | bytes accessed | tf_op | source)
XLA Modules:
  0.0 30.0 jit_solution(6583905952910769003)
XLA Ops:
  0.0 28.0 %shard_map.46 = f32[8,64,16,128]{3,2,1,0:T(8,128)S(1)} custom-call(f32[8,64,16,128]{3,2,1,0:T(8,128)} %sub_ref.1, f32[64,16,128]{2,1,0:T(8,128)} %up_ref.1, f32[8]{0:T(128)} %dif_hbm.1, f32[8]{0:T(128)} %dec_hbm.1), custom_call_target="tpu_custom_call" | custom-call | tf_op jit(solution)/shard_map/pallas_call | solution.py:196
  28.0 2.0 %copy.6 = f32[8,64,16,128]{3,2,1,0:T(8,128)} copy(f32[8,64,16,128]{3,2,1,0:T(8,128)S(1)} %shard_map.46) | data formatting | bytes 8388608

commit v3 on v2

--- a/solution.py
+++ b/solution.py
@@ -161,7 +161,7 @@
     for first, last, group in ((0, EARLY, 0), (EARLY, count, 1)):
         await_rows((last - first) * shell, front_sem.at[group])
         run(first, last, launch)
-    for k, other in enumerate(along_x):
+    for k, other in ((1, high_x), (0, low_x)):
 
         @pl.when(other > gx)
         def _():

time: 30.3 us -> 30 us (0.990)
  no operation moved by 1% of the time
where the time goes in v3:
time: 30 us; the launch traced here: 29.9 us
  Pallas kernels  27.9 us (93%)
  local copies, waits for them, and re-layouts  2.02 us (7%)
    pallas_call x1, Pallas kernels, local(): pl.pallas_call(functools.partial(kernel, n_x, n_y), out_shape=jax.ShapeDt...  27.9 us
    unnamed x1, local copies, waits for them, and re-layouts  2.02 us

profile of v3, /device:TPU:0, one launch (start us, length us, event | category | flops | bytes accessed | tf_op | source)
XLA Modules:
  0.0 29.9 jit_solution(182919963344298035)
XLA Ops:
  0.0 27.9 %shard_map.46 = f32[8,64,16,128]{3,2,1,0:T(8,128)S(1)} custom-call(f32[8,64,16,128]{3,2,1,0:T(8,128)} %sub_ref.1, f32[64,16,128]{2,1,0:T(8,128)} %up_ref.1, f32[8]{0:T(128)} %dif_hbm.1, f32[8]{0:T(128)} %dec_hbm.1), custom_call_target="tpu_custom_call" | custom-call | tf_op jit(solution)/shard_map/pallas_call | solution.py:196
  27.9 2.0 %copy.6 = f32[8,64,16,128]{3,2,1,0:T(8,128)} copy(f32[8,64,16,128]{3,2,1,0:T(8,128)S(1)} %shard_map.46) | data formatting | bytes 8388608

commit v4 on v3

--- a/solution.py
+++ b/solution.py
@@ -16,11 +16,12 @@
 
 def kernel(
     n_x, n_y, sub_ref, up_ref, dif_hbm, dec_hbm, out_ref,
-    field, uptake, faces, halos, front_sem, bulk_sem, up_sem, send_sem, recv_sem,
-    dif_ref, dec_ref, scalar_sem, ready,
+    field, uptake, faces, halos, front_sem, bulk_sem, send_sem, recv_sem,
+    dif_ref, dec_ref, ready,
 ):
     count, cx, cy, cz = sub_ref.shape
     pitch = cy + PITCH_PAD
+    out_rows = out_ref.reshape(count, cx * cy, cz)
     rows = field.reshape(SUBSTEPS, count, (cx + 2) * pitch, cz)
     gx, gy = lax.axis_index("gx"), lax.axis_index("gy")
     low_x, high_x = lax.rem(gx + n_x - 1, n_x), lax.rem(gx + 1, n_x)
@@ -51,7 +52,7 @@
 
     def remote(t, s, src, dst, target):
         return pltpu.make_async_remote_copy(
-            src_ref=src, dst_ref=dst, send_sem=send_sem.at[t],
+            src_ref=src, dst_ref=dst, send_sem=send_sem,
             recv_sem=recv_sem.at[t % 2, s], device_id=target, device_id_type=MESH,
         )
 
@@ -66,9 +67,6 @@
         if k == 0:
             return remote(t, s, here.at[1, inner, :], here.at[cx + 1, inner, :], (low_x, gy))
         return remote(t, s, here.at[cx, inner, :], here.at[0, inner, :], (high_x, gy))
-
-    def sends(t, s):
-        return y_sends(t, s) + [x_send(t, s, 0), x_send(t, s, 1)]
 
     def make_faces(t, s):
         for i in range(cx // 8):
@@ -78,25 +76,29 @@
                 t, s, pl.ds(top + cy - 1, 8, stride=pitch), :
             ]
 
-    def unit(t, s):
-        await_rows(shell, recv_sem.at[t % 2, s])
-        for i in range(cx // 8):
-            top = (1 + 8 * i) * pitch + Y0
-            rows[t, s, pl.ds(top + cy, 8, stride=pitch), :] = halos[t, s, 0, pl.ds(8 * i, 8), :]
-            rows[t, s, pl.ds(top - 1, 8, stride=pitch), :] = halos[t, s, 1, pl.ds(8 * i, 8), :]
+    def step(t, s, ghosts, first=0, last=None):
+        last = cx if last is None else last
         diffuse = dif_ref[s]
         keep = 1.0 - 6.0 * diffuse
         decay = dec_ref[s]
+        zero = jnp.zeros((8, cz), jnp.float32)
+        sublane = lax.broadcasted_iota(jnp.int32, (8, cz), 0)
         for y in range(0, cy, 8):
-            below = field[t, s, 0, pl.ds(Y0 + y, 8), :]
-            center = field[t, s, 1, pl.ds(Y0 + y, 8), :]
-            for x in range(cx):
-                above = field[t, s, x + 2, pl.ds(Y0 + y, 8), :]
+            below = field[t, s, first, pl.ds(Y0 + y, 8), :] if ghosts else zero
+            center = field[t, s, first + 1, pl.ds(Y0 + y, 8), :]
+            for x in range(first, last):
+                if ghosts or x + 1 < cx:
+                    above = field[t, s, x + 2, pl.ds(Y0 + y, 8), :]
+                else:
+                    above = zero
                 total = below + above
-                total = total + (
-                    field[t, s, x + 1, pl.ds(Y0 + y - 1, 8), :]
-                    + field[t, s, x + 1, pl.ds(Y0 + y + 1, 8), :]
-                )
+                left = field[t, s, x + 1, pl.ds(Y0 + y - 1, 8), :]
+                right = field[t, s, x + 1, pl.ds(Y0 + y + 1, 8), :]
+                if not ghosts and y == 0:
+                    left = jnp.where(sublane == 0, 0.0, left)
+                if not ghosts and y + 8 == cy:
+                    right = jnp.where(sublane == 7, 0.0, right)
+                total = total + (left + right)
                 total = total + (pltpu.roll(center, 1, 1) + pltpu.roll(center, cz - 1, 1))
                 factor = keep - decay * uptake[x, pl.ds(y, 8), :]
                 value = diffuse * total + factor * center
@@ -106,6 +108,32 @@
                     out_ref[s, x, pl.ds(y, 8), :] = value
                 below, center = center, above
 
+    def unit(t, s):
+        await_rows(shell, recv_sem.at[t % 2, s])
+        for i in range(cx // 8):
+            top = (1 + 8 * i) * pitch + Y0
+            rows[t, s, pl.ds(top + cy, 8, stride=pitch), :] = halos[t, s, 0, pl.ds(8 * i, 8), :]
+            rows[t, s, pl.ds(top - 1, 8, stride=pitch), :] = halos[t, s, 1, pl.ds(8 * i, 8), :]
+        step(t, s, True, 0, 1)
+        step(t, s, True, cx - 1, cx)
+        for k in range(2):
+            x_send(t + 1, s, k).start()
+        step(t, s, True, 1, cx - 1)
+        make_faces(t + 1, s)
+        for copy in y_sends(t + 1, s):
+            copy.start()
+
+    def last_unit(t, s):
+        step(t, s, False)
+        await_rows(shell, recv_sem.at[t % 2, s])
+        diffuse = dif_ref[s]
+        for x, ghost in ((0, 0), (cx - 1, cx + 1)):
+            out_ref[s, x] += diffuse * field[t, s, ghost, inner, :]
+        for i in range(cx // 8):
+            for k, y in ((0, cy - 1), (1, 0)):
+                edge = pl.ds(8 * i * cy + y, 8, stride=cy)
+                out_rows[s, edge, :] += diffuse * halos[t, s, k, pl.ds(8 * i, 8), :]
+
     def run(first, last, body):
         def wrapped(s, carry):
             body(s)
@@ -129,15 +157,8 @@
                 copy.start()
 
         run(first, last, begin)
-    scalar_copies = [
-        pltpu.make_async_copy(dif_hbm, dif_ref, scalar_sem.at[0]),
-        pltpu.make_async_copy(dec_hbm, dec_ref, scalar_sem.at[1]),
-    ]
-    for copy in scalar_copies:
-        copy.start()
     run(0, count, lambda s: bulk(s).start())
-    up_copy = pltpu.make_async_copy(up_ref, uptake, up_sem)
-    up_copy.start()
+    pltpu.make_async_copy(up_ref, uptake, bulk_sem).start()
 
     def launch(s):
         for copy in y_sends(0, s):
@@ -161,6 +182,12 @@
     for first, last, group in ((0, EARLY, 0), (EARLY, count, 1)):
         await_rows((last - first) * shell, front_sem.at[group])
         run(first, last, launch)
+    scalar_copies = [
+        pltpu.make_async_copy(dif_hbm, dif_ref, front_sem.at[0]),
+        pltpu.make_async_copy(dec_hbm, dec_ref, front_sem.at[1]),
+    ]
+    for copy in scalar_copies:
+        copy.start()
     for k, other in ((1, high_x), (0, low_x)):
 
         @pl.when(other > gx)
@@ -168,23 +195,13 @@
             pl.semaphore_wait(ready.at[k], 1)
             run(0, count, lambda s: x_send(0, s, k).start())
 
-    await_rows(count * (cx - 2) * cy, bulk_sem)
-    up_copy.wait()
+    await_rows(count * (cx - 2) * cy + cx * cy, bulk_sem)
     for copy in scalar_copies:
         copy.wait()
-    for t in range(SUBSTEPS):
-
-        def advance(s):
-            unit(t, s)
-            if t + 1 < SUBSTEPS:
-                make_faces(t + 1, s)
-                for copy in sends(t + 1, s):
-                    copy.start()
-
-        run(0, count, advance)
-
-    for t in range(SUBSTEPS):
-        await_rows(count * shell, send_sem.at[t])
+    for t in range(SUBSTEPS - 1):
+        run(0, count, lambda s: unit(t, s))
+    run(0, count, lambda s: last_unit(SUBSTEPS - 1, s))
+    await_rows(SUBSTEPS * count * shell, send_sem)
 
 
 def solution(mesh):
@@ -206,11 +223,9 @@
                 pltpu.SemaphoreType.DMA((2,)),
                 pltpu.SemaphoreType.DMA,
                 pltpu.SemaphoreType.DMA,
-                pltpu.SemaphoreType.DMA((SUBSTEPS,)),
                 pltpu.SemaphoreType.DMA((2, count)),
                 pltpu.SMEM((count,), jnp.float32),
                 pltpu.SMEM((count,), jnp.float32),
-                pltpu.SemaphoreType.DMA((2,)),
                 pltpu.SemaphoreType.REGULAR((2,)),
             ],
             compiler_params=pltpu.CompilerParams(

time: 30 us -> 29.6 us (0.987)
  Pallas kernels: 27.9 us -> 27.4 us
    pallas_call x1, Pallas kernels: 27.9 us -> 27.4 us  [local(): pl.pallas_call(functools.partial(kernel, n_x, n_y), out_shape=jax.ShapeDt...]
where the time goes in v4:
time: 29.6 us; the launch traced here: 29.4 us
  Pallas kernels  27.4 us (93%)
  local copies, waits for them, and re-layouts  2.02 us (7%)
    pallas_call x1, Pallas kernels, local(): pl.pallas_call(functools.partial(kernel, n_x, n_y), out_shape=jax.ShapeDt...  27.4 us
    unnamed x1, local copies, waits for them, and re-layouts  2.02 us

profile of v4, /device:TPU:0, one launch (start us, length us, event | category | flops | bytes accessed | tf_op | source)
XLA Modules:
  0.0 29.4 jit_solution(6035011253106356652)
XLA Ops:
  0.0 27.4 %shard_map.46 = f32[8,64,16,128]{3,2,1,0:T(8,128)S(1)} custom-call(f32[8,64,16,128]{3,2,1,0:T(8,128)} %sub_ref.1, f32[64,16,128]{2,1,0:T(8,128)} %up_ref.1, f32[8]{0:T(128)} %dif_hbm.1, f32[8]{0:T(128)} %dec_hbm.1), custom_call_target="tpu_custom_call" | custom-call | tf_op jit(solution)/shard_map/pallas_call | solution.py:213
  27.4 2.0 %copy.6 = f32[8,64,16,128]{3,2,1,0:T(8,128)} copy(f32[8,64,16,128]{3,2,1,0:T(8,128)S(1)} %shard_map.46) | data formatting | bytes 8388608

commit v5 on v4

--- a/solution.py
+++ b/solution.py
@@ -11,6 +11,7 @@
 PITCH_PAD = 16
 Y0 = 8
 EARLY = 2
+LAG = 3
 MESH = pl.DeviceIdType.MESH
 
 
@@ -108,7 +109,26 @@
                     out_ref[s, x, pl.ds(y, 8), :] = value
                 below, center = center, above
 
+    upward = jnp.logical_and(lax.rem(gy, 2) == 1, gy < n_y - 1)
+    yielding = {
+        (SUBSTEPS - 2, 1): (upward, LAG),
+        (SUBSTEPS - 1, 1): (upward, LAG),
+        (SUBSTEPS - 1, 0): (gy == n_y - 2, LAG + 1),
+    }
+
+    def send_if(condition, t, s, k):
+        @pl.when(condition)
+        def _():
+            y_sends(t, s)[k].start()
+
+    def send_lagging(t, s):
+        for k in range(2):
+            if (t, k) in yielding:
+                give_way, lag = yielding[t, k]
+                send_if(jnp.logical_and(give_way, s < lag), t, count - lag + s, k)
+
     def unit(t, s):
+        send_lagging(t, s)
         await_rows(shell, recv_sem.at[t % 2, s])
         for i in range(cx // 8):
             top = (1 + 8 * i) * pitch + Y0
@@ -120,10 +140,16 @@
             x_send(t + 1, s, k).start()
         step(t, s, True, 1, cx - 1)
         make_faces(t + 1, s)
-        for copy in y_sends(t + 1, s):
-            copy.start()
+        for k in range(2):
+            if (t + 1, k) in yielding:
+                give_way, lag = yielding[t + 1, k]
+                send_if(jnp.logical_not(give_way), t + 1, s, k)
+                send_if(jnp.logical_and(give_way, s >= lag), t + 1, s - lag, k)
+            else:
+                y_sends(t + 1, s)[k].start()
 
     def last_unit(t, s):
+        send_lagging(t, s)
         step(t, s, False)
         await_rows(shell, recv_sem.at[t % 2, s])
         diffuse = dif_ref[s]

time: 29.6 us -> 29.5 us (level)
  no operation moved by 1% of the time
where the time goes in v5:
time: 29.5 us; the launch traced here: 29.3 us
  Pallas kernels  27.3 us (93%)
  local copies, waits for them, and re-layouts  2.02 us (7%)
    pallas_call x1, Pallas kernels, local(): pl.pallas_call(functools.partial(kernel, n_x, n_y), out_shape=jax.ShapeDt...  27.3 us
    unnamed x1, local copies, waits for them, and re-layouts  2.02 us

profile of v5, /device:TPU:0, one launch (start us, length us, event | category | flops | bytes accessed | tf_op | source)
XLA Modules:
  0.0 29.3 jit_solution(15799529984815359995)
XLA Ops:
  0.0 27.3 %shard_map.46 = f32[8,64,16,128]{3,2,1,0:T(8,128)S(1)} custom-call(f32[8,64,16,128]{3,2,1,0:T(8,128)} %sub_ref.1, f32[64,16,128]{2,1,0:T(8,128)} %up_ref.1, f32[8]{0:T(128)} %dif_hbm.1, f32[8]{0:T(128)} %dec_hbm.1), custom_call_target="tpu_custom_call" | custom-call | tf_op jit(solution)/shard_map/pallas_call | solution.py:239
  27.3 2.0 %copy.6 = f32[8,64,16,128]{3,2,1,0:T(8,128)} copy(f32[8,64,16,128]{3,2,1,0:T(8,128)S(1)} %shard_map.46) | data formatting | bytes 8388608

commit v6 on v5

--- a/solution.py
+++ b/solution.py
@@ -113,6 +113,7 @@
     yielding = {
         (SUBSTEPS - 2, 1): (upward, LAG),
         (SUBSTEPS - 1, 1): (upward, LAG),
+        (SUBSTEPS - 2, 0): (gy == n_y - 2, LAG),
         (SUBSTEPS - 1, 0): (gy == n_y - 2, LAG + 1),
     }
 
@@ -130,14 +131,19 @@
     def unit(t, s):
         send_lagging(t, s)
         await_rows(shell, recv_sem.at[t % 2, s])
-        for i in range(cx // 8):
+        def place(i):
             top = (1 + 8 * i) * pitch + Y0
             rows[t, s, pl.ds(top + cy, 8, stride=pitch), :] = halos[t, s, 0, pl.ds(8 * i, 8), :]
             rows[t, s, pl.ds(top - 1, 8, stride=pitch), :] = halos[t, s, 1, pl.ds(8 * i, 8), :]
+
+        place(0)
+        place(cx // 8 - 1)
         step(t, s, True, 0, 1)
         step(t, s, True, cx - 1, cx)
         for k in range(2):
             x_send(t + 1, s, k).start()
+        for i in range(1, cx // 8 - 1):
+            place(i)
         step(t, s, True, 1, cx - 1)
         make_faces(t + 1, s)
         for k in range(2):

time: 29.5 us -> 29.4 us (level)
  no operation moved by 1% of the time
where the time goes in v6:
time: 29.4 us; the launch traced here: 29.2 us
  Pallas kernels  27.2 us (93%)
  local copies, waits for them, and re-layouts  2.02 us (7%)
    pallas_call x1, Pallas kernels, local(): pl.pallas_call(functools.partial(kernel, n_x, n_y), out_shape=jax.ShapeDt...  27.2 us
    unnamed x1, local copies, waits for them, and re-layouts  2.02 us

profile of v6, /device:TPU:0, one launch (start us, length us, event | category | flops | bytes accessed | tf_op | source)
XLA Modules:
  0.0 29.2 jit_solution(15418732517463165556)
XLA Ops:
  0.0 27.2 %shard_map.46 = f32[8,64,16,128]{3,2,1,0:T(8,128)S(1)} custom-call(f32[8,64,16,128]{3,2,1,0:T(8,128)} %sub_ref.1, f32[64,16,128]{2,1,0:T(8,128)} %up_ref.1, f32[8]{0:T(128)} %dif_hbm.1, f32[8]{0:T(128)} %dec_hbm.1), custom_call_target="tpu_custom_call" | custom-call | tf_op jit(solution)/shard_map/pallas_call | solution.py:245
  27.2 2.0 %copy.6 = f32[8,64,16,128]{3,2,1,0:T(8,128)} copy(f32[8,64,16,128]{3,2,1,0:T(8,128)S(1)} %shard_map.46) | data formatting | bytes 8388608

commit v7 on v6

--- a/solution.py
+++ b/solution.py
@@ -140,7 +140,7 @@
         place(cx // 8 - 1)
         step(t, s, True, 0, 1)
         step(t, s, True, cx - 1, cx)
-        for k in range(2):
+        for k in (1, 0):
             x_send(t + 1, s, k).start()
         for i in range(1, cx // 8 - 1):
             place(i)

time: 29.4 us -> 29.3 us (level)
  no operation moved by 1% of the time
where the time goes in v7:
time: 29.3 us; the launch traced here: 29.1 us
  Pallas kernels  27.1 us (92%)
  local copies, waits for them, and re-layouts  2.02 us (7%)
    pallas_call x1, Pallas kernels, local(): pl.pallas_call(functools.partial(kernel, n_x, n_y), out_shape=jax.ShapeDt...  27.1 us
    unnamed x1, local copies, waits for them, and re-layouts  2.02 us

profile of v7, /device:TPU:0, one launch (start us, length us, event | category | flops | bytes accessed | tf_op | source)
XLA Modules:
  0.0 29.1 jit_solution(15431274224066328049)
XLA Ops:
  0.0 27.1 %shard_map.46 = f32[8,64,16,128]{3,2,1,0:T(8,128)S(1)} custom-call(f32[8,64,16,128]{3,2,1,0:T(8,128)} %sub_ref.1, f32[64,16,128]{2,1,0:T(8,128)} %up_ref.1, f32[8]{0:T(128)} %dif_hbm.1, f32[8]{0:T(128)} %dec_hbm.1), custom_call_target="tpu_custom_call" | custom-call | tf_op jit(solution)/shard_map/pallas_call | solution.py:245
  27.1 2.0 %copy.6 = f32[8,64,16,128]{3,2,1,0:T(8,128)} copy(f32[8,64,16,128]{3,2,1,0:T(8,128)S(1)} %shard_map.46) | data formatting | bytes 8388608

commit v8 on v7

--- a/solution.py
+++ b/solution.py
@@ -113,7 +113,7 @@
     yielding = {
         (SUBSTEPS - 2, 1): (upward, LAG),
         (SUBSTEPS - 1, 1): (upward, LAG),
-        (SUBSTEPS - 2, 0): (gy == n_y - 2, LAG),
+        (SUBSTEPS - 2, 0): (gy == n_y - 2, LAG - 1),
         (SUBSTEPS - 1, 0): (gy == n_y - 2, LAG + 1),
     }
 

time: 29.3 us -> 29.3 us (level)
  no operation moved by 1% of the time
where the time goes in v8:
time: 29.3 us; the launch traced here: 29.2 us
  Pallas kernels  27.1 us (92%)
  local copies, waits for them, and re-layouts  2.02 us (7%)
    pallas_call x1, Pallas kernels, local(): pl.pallas_call(functools.partial(kernel, n_x, n_y), out_shape=jax.ShapeDt...  27.1 us
    unnamed x1, local copies, waits for them, and re-layouts  2.02 us

profile of v8, /device:TPU:0, one launch (start us, length us, event | category | flops | bytes accessed | tf_op | source)
XLA Modules:
  0.0 29.2 jit_solution(17390150543245590054)
XLA Ops:
  0.0 27.1 %shard_map.46 = f32[8,64,16,128]{3,2,1,0:T(8,128)S(1)} custom-call(f32[8,64,16,128]{3,2,1,0:T(8,128)} %sub_ref.1, f32[64,16,128]{2,1,0:T(8,128)} %up_ref.1, f32[8]{0:T(128)} %dif_hbm.1, f32[8]{0:T(128)} %dec_hbm.1), custom_call_target="tpu_custom_call" | custom-call | tf_op jit(solution)/shard_map/pallas_call | solution.py:245
  27.2 2.0 %copy.6 = f32[8,64,16,128]{3,2,1,0:T(8,128)} copy(f32[8,64,16,128]{3,2,1,0:T(8,128)S(1)} %shard_map.46) | data formatting | bytes 8388608
